TPU v7x, 32 devices: a whole 2x2x4 slice. The times are simulated.
32 devices in a mesh: wide: 8 (over z, x), narrow: 4 (over y, core).
Axes of the slice: x: 2, y: 2, z: 4, core: 2. Of those that a mesh axis runs over, the one named last changes fastest.
Arguments:
- payload: bfloat16 [131072, 128], P(('wide', 'narrow')), may hold values from -6 to 6
- first_key: int32 [131072], P(('wide', 'narrow')), may hold values from 0 to 1073741823
- second_key: int32 [131072], P(('wide', 'narrow')), may hold values from 0 to 1073741823
- live: int32 [131072], P(('wide', 'narrow')), may hold values from 0 to 1
- first_bucket: int32 [131072], P(('wide', 'narrow')), may hold values from 0 to 7, as said below
- second_bucket: int32 [131072], P(('wide', 'narrow')), may hold values from 0 to 3
Outputs:
- group_mean: bfloat16 [131072, 128], P(('wide', 'narrow'))
- duplicate_count: int32 [], replicated
Inputs may be any that keep to these rules, and one draw needn't show every extreme that they name: Each device's rows name each pair (first_bucket, second_bucket) exactly 128 times; in every draw there is one bucket pair all of whose rows survive; other rows survive or not as `live` says.
All inputs are finite; a program needn't handle non-finite values.
Results may differ from a plain program's by a relative error of at most 0.001.
Values may be sent and summed in bfloat16 or wider, within the bound.
A program may use at most 64 MiB of HBM per device.

v0:
```python
import jax
import jax.numpy as jnp
from jax import lax
from jax.sharding import PartitionSpec as P


def pair_mask(row_one, row_two, row_live, col_one, col_two, col_live):
    return (
        (row_one[:, None] == col_one[None, :])
        & (row_two[:, None] == col_two[None, :])
        & (row_live[:, None] > 0)
        & (col_live[None, :] > 0)
    )


def on_device(payload, first_key, second_key, live, first_bucket, second_bucket):
    wide_count = lax.axis_size("wide")
    narrow_count = lax.axis_size("narrow")
    row_count, feature_cols = payload.shape
    slot_rows = row_count // (wide_count * narrow_count)
    owner = first_bucket * narrow_count + second_bucket
    sort_order = jnp.argsort(owner, stable=True)
    inverse = jnp.argsort(sort_order, stable=True)
    sent_rows = payload[sort_order].reshape(wide_count, narrow_count, slot_rows, feature_cols)
    shaped = (wide_count, narrow_count, slot_rows)
    tags = jnp.stack(
        [
            first_key[sort_order].reshape(shaped),
            second_key[sort_order].reshape(shaped),
            live[sort_order].reshape(shaped),
        ],
        axis=2,
    )
    got_rows, got_tags = (
        lax.all_to_all(
            lax.all_to_all(sent_rows, "wide", split_axis=0, concat_axis=0, tiled=True),
            "narrow",
            split_axis=1,
            concat_axis=1,
            tiled=True,
        ),
        lax.all_to_all(
            lax.all_to_all(tags, "wide", split_axis=0, concat_axis=0, tiled=True),
            "narrow",
            split_axis=1,
            concat_axis=1,
            tiled=True,
        ),
    )
    owner_rows = wide_count * narrow_count * slot_rows
    flat_rows = got_rows.reshape(owner_rows, feature_cols)
    keys_one = got_tags[:, :, 0, :].reshape(owner_rows)
    keys_two = got_tags[:, :, 1, :].reshape(owner_rows)
    alive = got_tags[:, :, 2, :].reshape(owner_rows)
    tile_rows = min(512, owner_rows)
    column_pos = lax.iota(jnp.int32, owner_rows)

    def full_block(block_index, running):
        group_means, duplicate_total = running
        block_start = block_index * tile_rows
        row_one = lax.dynamic_slice_in_dim(keys_one, block_start, tile_rows)
        row_two = lax.dynamic_slice_in_dim(keys_two, block_start, tile_rows)
        row_live = lax.dynamic_slice_in_dim(alive, block_start, tile_rows)
        same = pair_mask(row_one, row_two, row_live, keys_one, keys_two, alive)
        sums = jnp.dot(same.astype(jnp.bfloat16), flat_rows, preferred_element_type=jnp.float32)
        counts = jnp.sum(same.astype(jnp.float32), axis=1)
        row_pos = block_start + lax.iota(jnp.int32, tile_rows)
        earlier = same & (column_pos[None, :] < row_pos[:, None])
        duplicate_total = duplicate_total + jnp.sum(jnp.any(earlier, axis=1).astype(jnp.float32))
        block_mean = (sums / jnp.maximum(counts, 1.0)[:, None]).astype(jnp.bfloat16)
        group_means = lax.dynamic_update_slice_in_dim(group_means, block_mean, block_start, 0)
        return (group_means, duplicate_total)

    start_state = (jnp.zeros((owner_rows, feature_cols), jnp.bfloat16), jnp.zeros((), jnp.float32))
    group_means, duplicate_total = lax.fori_loop(
        0, owner_rows // tile_rows, full_block, start_state
    )
    back_rows = group_means.reshape(wide_count, narrow_count, slot_rows, feature_cols)
    returned = lax.all_to_all(
        lax.all_to_all(back_rows, "wide", split_axis=0, concat_axis=0, tiled=True),
        "narrow",
        split_axis=1,
        concat_axis=1,
        tiled=True,
    )
    group_mean = returned.reshape(row_count, feature_cols)[inverse]
    overall = lax.psum(duplicate_total, ("wide", "narrow"))
    return (group_mean, overall.astype(jnp.int32))


def solution(mesh):
    placed = (
        P(("wide", "narrow"), None),
        P(("wide", "narrow")),
        P(("wide", "narrow")),
        P(("wide", "narrow")),
        P(("wide", "narrow")),
        P(("wide", "narrow")),
    )
    return jax.shard_map(
        on_device,
        mesh=mesh,
        in_specs=placed,
        out_specs=(P(("wide", "narrow"), None), P()),
        check_vma=False,
    )
```

profile of v0, /device:TPU:0, one launch (start us, length us, event | category | flops | bytes accessed | tf_op | source)
XLA Modules:
  0.0 326.9 jit_solution(6354122044880662689)
XLA Ops:
  0.7 0.8 multiply_add_fusion
  1.5 5.8 %sort.31 = (s32[4096]{0:T(1024)}, s32[4096]{0:T(1024)S(1)}) sort(s32[4096]{0:T(1024)S(1)} %multiply_add_fusion, s32[4096]{0:T(1024)S(1)} %iota.19), dimensions={0}, to_apply=%region_0.0 | sort | flops 49152 | bytes 65536 | tf_op jit(solution)/shard_map/jit(argsort)/sort | solution.py:22
  7.3 23.0 %gather_fusion.2 = s32[4096]{0:T(1024)S(1)} fusion(s32[4096]{0:T(1024)S(1)} %copy-done.1, s32[4096]{0:T(1024)S(1)} %fusion.6), kind=kCustom, calls=%fused_computation.2 | custom fusion | bytes 49152 | tf_op jit(solution)/shard_map/gather | solution.py:30
  30.4 23.0 %gather_fusion.1 = s32[4096]{0:T(1024)S(1)} fusion(s32[4096]{0:T(1024)S(1)} %copy-done.2, s32[4096]{0:T(1024)S(1)} %fusion.6), kind=kCustom, calls=%fused_computation.1 | custom fusion | bytes 49152 | tf_op jit(solution)/shard_map/gather | solution.py:29
  53.4 23.0 %gather_fusion = s32[4096]{0:T(1024)S(1)} fusion(s32[4096]{0:T(1024)S(1)} %copy-done.3, s32[4096]{0:T(1024)S(1)} %fusion.6), kind=kCustom, calls=%fused_computation | custom fusion | bytes 49152 | tf_op jit(solution)/shard_map/gather | solution.py:28
  76.4 0.6 pad_add_fusion
  77.1 7.3 %all-to-all-start = ((s32[8,4,3,128]{3,1,2,0:T(4,128)}), s32[8,4,3,128]{3,1,2,0:T(4,128)S(1)}, u32[]{:S(2)}, u32[]{:S(2)}) async-start(s32[8,4,3,128]{3,1,2,0:T(4,128)} %pad_add_fusion), calls=%async_computation | async-start | bytes 98304 | tf_op jit(solution)/shard_map/all_to_all | solution.py:43
  84.4 15.0 %gather_fusion.3 = bf16[4096,128]{1,0:T(8,128)(2,1)} fusion(bf16[4096,128]{1,0:T(8,128)(2,1)S(1)} %copy-done, s32[4096]{0:T(1024)S(1)} %fusion.6), kind=kCustom, calls=%fused_computation.3 | custom fusion | bytes 2113536 | tf_op jit(solution)/shard_map/gather | solution.py:24
  99.4 6.0 %all-to-all-start.2 = ((bf16[8,4,128,128]{3,2,1,0:T(8,128)(2,1)}), bf16[8,4,128,128]{3,2,1,0:T(8,128)(2,1)S(1)}, u32[]{:S(2)}, u32[]{:S(2)}) async-start(bf16[8,4,128,128]{3,2,1,0:T(8,128)(2,1)} %bitcast.6), calls=%async_computation.2 | async-start | bytes 2097152 | tf_op jit(solution)/shard_map/all_to_all | solution.py:36
  105.4 0.6 copy.38
  106.0 24.8 %all-to-all-done.2 = bf16[8,4,128,128]{3,2,1,0:T(8,128)(2,1)S(1)} async-done(((bf16[8,4,128,128]{3,2,1,0:T(8,128)(2,1)}), bf16[8,4,128,128]{3,2,1,0:T(8,128)(2,1)S(1)}, u32[]{:S(2)}, u32[]{:S(2)}) %all-to-all-start.2) | async-done | bytes 1048608 | tf_op jit(solution)/shard_map/all_to_all | solution.py:36
  130.8 3.3 %all-to-all-start.1 = ((s32[8,4,3,128]{3,0,2,1:T(8,128)}), s32[8,4,3,128]{3,0,2,1:T(8,128)S(1)}, u32[]{:S(2)}, u32[]{:S(2)}) async-start(s32[8,4,3,128]{3,0,2,1:T(8,128)} %copy.38), calls=%async_computation.1 | async-start | bytes 98304 | tf_op jit(solution)/shard_map/all_to_all | solution.py:42
  134.1 1.0 copy.42
  135.1 3.0 all-to-all-done.1
  138.1 3.5 %all-to-all-start.3 = ((bf16[8,4,128,128]{3,2,0,1:T(8,128)(2,1)}), bf16[8,4,128,128]{3,2,0,1:T(8,128)(2,1)S(1)}, u32[]{:S(2)}, u32[]{:S(2)}) async-start(bf16[8,4,128,128]{3,2,0,1:T(8,128)(2,1)} %copy.42), calls=%async_computation.3 | async-start | bytes 2097152 | tf_op jit(solution)/shard_map/all_to_all | solution.py:35
  141.7 14.3 %all-to-all-done.3 = bf16[8,4,128,128]{3,2,0,1:T(8,128)(2,1)S(1)} async-done(((bf16[8,4,128,128]{3,2,0,1:T(8,128)(2,1)}), bf16[8,4,128,128]{3,2,0,1:T(8,128)(2,1)S(1)}, u32[]{:S(2)}, u32[]{:S(2)}) %all-to-all-start.3) | async-done | bytes 1048608 | tf_op jit(solution)/shard_map/all_to_all | solution.py:35
  156.0 1.1 copy.43
  157.1 1.1 broadcast_in_dim.30
  158.2 71.2 %while.16 = (s32[]{:T(128)}, bf16[4096,128]{1,0:T(8,128)(2,1)}, f32[]{:T(128)}, s32[4096]{0:T(1024)S(1)}, s32[8,4,1,128]{3,2,1,0:T(1,128)S(1)}, /*index=5*/s32[4...) while((s32[]{:T(128)}, bf16[4096,128]{1,0:T(8,128)(2,1)}, ...), condition=%wide.region_5.6_spmd.clone, body=%wide.region_1.5_spmd.clone.sunk | while | flops 557979136 | bytes 11751667 | solution.py:75
  158.4 4.1 %fusion.17 = (pred[512]{0:T(512)(128)(4,1)S(1)}, pred[512,4096]{1,0:T(32,128)(4,1)S(1)}) fusion(s32[512]{0:T(512)S(1)} %iota_add_fusion.2, pred[4096]{0:T(1024)(128)(4,1)S(1)} %bitcast.33, pred[512]{0:T(512)(128)(4,1)S(1)} %dynamic-slice_compare_fusion.2, s32[4096]{0:T(1024)S(1)} %bitcast.31, s32[512]{0:T(512)S(1)} %dynamic_slice.29, ...), kind=kLoop, calls=%fused_computation.9.clone.1 | loop fusion | flops 16776704 | bytes 2141184 | tf_op jit(solution)/shard_map/while/body/eval_jaxpr/reduce_or | solution.py:69
  162.6 0.7 convert_reduce_fusion.5
  164.0 1.0 convert_reduce_fusion.4
  164.9 0.2 copy-done.4
  165.2 1.9 fusion.18
  167.3 4.1 %fusion.17 = (pred[512]{0:T(512)(128)(4,1)S(1)}, pred[512,4096]{1,0:T(32,128)(4,1)S(1)}) fusion(s32[512]{0:T(512)S(1)} %iota_add_fusion.2, pred[4096]{0:T(1024)(128)(4,1)S(1)} %bitcast.33, pred[512]{0:T(512)(128)(4,1)S(1)} %dynamic-slice_compare_fusion.2, s32[4096]{0:T(1024)S(1)} %bitcast.31, s32[512]{0:T(512)S(1)} %dynamic_slice.29, ...), kind=kLoop, calls=%fused_computation.9.clone.1 | loop fusion | flops 16776704 | bytes 2141184 | tf_op jit(solution)/shard_map/while/body/eval_jaxpr/reduce_or | solution.py:69
  171.5 0.7 convert_reduce_fusion.5
  172.9 1.0 convert_reduce_fusion.4
  173.8 0.2 copy-done.4
  174.1 1.9 fusion.18
  176.2 4.1 %fusion.17 = (pred[512]{0:T(512)(128)(4,1)S(1)}, pred[512,4096]{1,0:T(32,128)(4,1)S(1)}) fusion(s32[512]{0:T(512)S(1)} %iota_add_fusion.2, pred[4096]{0:T(1024)(128)(4,1)S(1)} %bitcast.33, pred[512]{0:T(512)(128)(4,1)S(1)} %dynamic-slice_compare_fusion.2, s32[4096]{0:T(1024)S(1)} %bitcast.31, s32[512]{0:T(512)S(1)} %dynamic_slice.29, ...), kind=kLoop, calls=%fused_computation.9.clone.1 | loop fusion | flops 16776704 | bytes 2141184 | tf_op jit(solution)/shard_map/while/body/eval_jaxpr/reduce_or | solution.py:69
  180.4 0.7 convert_reduce_fusion.5
  181.8 1.0 convert_reduce_fusion.4
  182.7 0.2 copy-done.4
  183.0 1.9 fusion.18
  185.1 4.1 %fusion.17 = (pred[512]{0:T(512)(128)(4,1)S(1)}, pred[512,4096]{1,0:T(32,128)(4,1)S(1)}) fusion(s32[512]{0:T(512)S(1)} %iota_add_fusion.2, pred[4096]{0:T(1024)(128)(4,1)S(1)} %bitcast.33, pred[512]{0:T(512)(128)(4,1)S(1)} %dynamic-slice_compare_fusion.2, s32[4096]{0:T(1024)S(1)} %bitcast.31, s32[512]{0:T(512)S(1)} %dynamic_slice.29, ...), kind=kLoop, calls=%fused_computation.9.clone.1 | loop fusion | flops 16776704 | bytes 2141184 | tf_op jit(solution)/shard_map/while/body/eval_jaxpr/reduce_or | solution.py:69
  189.3 0.7 convert_reduce_fusion.5
  190.7 1.0 convert_reduce_fusion.4
  191.6 0.2 copy-done.4
  191.9 1.9 fusion.18
  194.0 4.1 %fusion.17 = (pred[512]{0:T(512)(128)(4,1)S(1)}, pred[512,4096]{1,0:T(32,128)(4,1)S(1)}) fusion(s32[512]{0:T(512)S(1)} %iota_add_fusion.2, pred[4096]{0:T(1024)(128)(4,1)S(1)} %bitcast.33, pred[512]{0:T(512)(128)(4,1)S(1)} %dynamic-slice_compare_fusion.2, s32[4096]{0:T(1024)S(1)} %bitcast.31, s32[512]{0:T(512)S(1)} %dynamic_slice.29, ...), kind=kLoop, calls=%fused_computation.9.clone.1 | loop fusion | flops 16776704 | bytes 2141184 | tf_op jit(solution)/shard_map/while/body/eval_jaxpr/reduce_or | solution.py:69
  198.2 0.7 convert_reduce_fusion.5
  199.6 1.0 convert_reduce_fusion.4
  200.5 0.2 copy-done.4
  200.8 1.9 fusion.18
  202.9 4.1 %fusion.17 = (pred[512]{0:T(512)(128)(4,1)S(1)}, pred[512,4096]{1,0:T(32,128)(4,1)S(1)}) fusion(s32[512]{0:T(512)S(1)} %iota_add_fusion.2, pred[4096]{0:T(1024)(128)(4,1)S(1)} %bitcast.33, pred[512]{0:T(512)(128)(4,1)S(1)} %dynamic-slice_compare_fusion.2, s32[4096]{0:T(1024)S(1)} %bitcast.31, s32[512]{0:T(512)S(1)} %dynamic_slice.29, ...), kind=kLoop, calls=%fused_computation.9.clone.1 | loop fusion | flops 16776704 | bytes 2141184 | tf_op jit(solution)/shard_map/while/body/eval_jaxpr/reduce_or | solution.py:69
  207.1 0.7 convert_reduce_fusion.5
  208.5 1.0 convert_reduce_fusion.4
  209.4 0.2 copy-done.4
  209.7 1.9 fusion.18
  211.9 4.1 %fusion.17 = (pred[512]{0:T(512)(128)(4,1)S(1)}, pred[512,4096]{1,0:T(32,128)(4,1)S(1)}) fusion(s32[512]{0:T(512)S(1)} %iota_add_fusion.2, pred[4096]{0:T(1024)(128)(4,1)S(1)} %bitcast.33, pred[512]{0:T(512)(128)(4,1)S(1)} %dynamic-slice_compare_fusion.2, s32[4096]{0:T(1024)S(1)} %bitcast.31, s32[512]{0:T(512)S(1)} %dynamic_slice.29, ...), kind=kLoop, calls=%fused_computation.9.clone.1 | loop fusion | flops 16776704 | bytes 2141184 | tf_op jit(solution)/shard_map/while/body/eval_jaxpr/reduce_or | solution.py:69
  216.0 0.7 convert_reduce_fusion.5
  217.4 1.0 convert_reduce_fusion.4
  218.6 1.9 fusion.18
  220.8 4.1 %fusion.17 = (pred[512]{0:T(512)(128)(4,1)S(1)}, pred[512,4096]{1,0:T(32,128)(4,1)S(1)}) fusion(s32[512]{0:T(512)S(1)} %iota_add_fusion.2, pred[4096]{0:T(1024)(128)(4,1)S(1)} %bitcast.33, pred[512]{0:T(512)(128)(4,1)S(1)} %dynamic-slice_compare_fusion.2, s32[4096]{0:T(1024)S(1)} %bitcast.31, s32[512]{0:T(512)S(1)} %dynamic_slice.29, ...), kind=kLoop, calls=%fused_computation.9.clone.1 | loop fusion | flops 16776704 | bytes 2141184 | tf_op jit(solution)/shard_map/while/body/eval_jaxpr/reduce_or | solution.py:69
  224.9 0.7 convert_reduce_fusion.5
  226.3 1.0 convert_reduce_fusion.4
  227.3 0.2 copy-done.4
  227.5 1.9 fusion.18
  229.4 29.2 %all_to_all.30 = bf16[8,4,128,128]{3,2,1,0:T(8,128)(2,1)S(1)} all-to-all(bf16[8,4,128,128]{3,2,1,0:T(8,128)(2,1)} %bitcast.26), channel_id=1, replica_groups=mesh['wide'=8,'narrow'=4] {'wide'}, dimensions={0} | all-to-all | bytes 2097152 | tf_op jit(solution)/shard_map/all_to_all | solution.py:80
  258.6 1.0 copy.47
  259.6 3.5 %all-to-all-start.5 = ((bf16[8,4,128,128]{3,2,0,1:T(8,128)(2,1)}), bf16[8,4,128,128]{3,2,0,1:T(8,128)(2,1)S(1)}, u32[]{:S(2)}, u32[]{:S(2)}) async-start(bf16[8,4,128,128]{3,2,0,1:T(8,128)(2,1)} %copy.47), calls=%async_computation.5 | async-start | bytes 2097152 | tf_op jit(solution)/shard_map/all_to_all | solution.py:79
  263.2 5.8 %sort.32 = (s32[4096]{0:T(1024)}, s32[4096]{0:T(1024)S(1)}) sort(s32[4096]{0:T(1024)S(1)} %get-tuple-element.189, s32[4096]{0:T(1024)S(1)} %iota.21), dimensions={0}, to_apply=%region_6.7 | sort | flops 49152 | bytes 65536 | tf_op jit(solution)/shard_map/jit(argsort)/sort | solution.py:23
  269.0 40.9 %psum.7 = f32[]{:T(128)} all-reduce(f32[]{:T(128)} %get-tuple-element.192), channel_id=1, replica_groups=mesh['wide'=8,'narrow'=4] {'wide','narrow'}, use_global_device_ids=true, to_apply=%region_7.8 | all-reduce | flops 1 | bytes 8 | tf_op jit(solution)/shard_map/psum | solution.py:87
  310.7 15.0 %gather_fusion.4 = bf16[4096,128]{1,0:T(8,128)(2,1)} fusion(bf16[4096,128]{1,0:T(8,128)(2,1)S(1)} %bitcast.25, s32[4096]{0:T(1024)S(1)} %fusion.7), kind=kCustom, calls=%fused_computation.4 | custom fusion | bytes 2113536 | tf_op jit(solution)/shard_map/gather | solution.py:86
  (78 shorter events, 2.4 us)
Async XLA Ops:
  0.6 83.7 %copy-start = (bf16[4096,128]{1,0:T(8,128)(2,1)S(1)}, bf16[4096,128]{1,0:T(8,128)(2,1)}, u32[]{:S(2)}) copy-start(bf16[4096,128]{1,0:T(8,128)(2,1)} %param.8) | copy-start | bytes 3145732
  0.6 6.6 %copy-start.1 = (s32[4096]{0:T(1024)S(1)}, s32[4096]{0:T(1024)}, u32[]{:S(2)}) copy-start(s32[4096]{0:T(1024)} %param.11) | copy-start | bytes 49156
  7.3 23.1 %copy-start.2 = (s32[4096]{0:T(1024)S(1)}, s32[4096]{0:T(1024)}, u32[]{:S(2)}) copy-start(s32[4096]{0:T(1024)} %param.10) | copy-start | bytes 49156
  30.3 23.1 %copy-start.3 = (s32[4096]{0:T(1024)S(1)}, s32[4096]{0:T(1024)}, u32[]{:S(2)}) copy-start(s32[4096]{0:T(1024)} %param.9) | copy-start | bytes 49156
  77.1 22.3 %all-to-all-start = ((s32[8,4,3,128]{3,1,2,0:T(4,128)}), s32[8,4,3,128]{3,1,2,0:T(4,128)S(1)}, u32[]{:S(2)}, u32[]{:S(2)}) async-start(s32[8,4,3,128]{3,1,2,0:T(4,128)} %pad_add_fusion), calls=%async_computation | async-start | bytes 98304 | tf_op jit(solution)/shard_map/all_to_all | solution.py:43
  99.4 31.4 %all-to-all-start.2 = ((bf16[8,4,128,128]{3,2,1,0:T(8,128)(2,1)}), bf16[8,4,128,128]{3,2,1,0:T(8,128)(2,1)S(1)}, u32[]{:S(2)}, u32[]{:S(2)}) async-start(bf16[8,4,128,128]{3,2,1,0:T(8,128)(2,1)} %bitcast.6), calls=%async_computation.2 | async-start | bytes 2097152 | tf_op jit(solution)/shard_map/all_to_all | solution.py:36
  130.8 7.3 %all-to-all-start.1 = ((s32[8,4,3,128]{3,0,2,1:T(8,128)}), s32[8,4,3,128]{3,0,2,1:T(8,128)S(1)}, u32[]{:S(2)}, u32[]{:S(2)}) async-start(s32[8,4,3,128]{3,0,2,1:T(8,128)} %copy.38), calls=%async_computation.1 | async-start | bytes 98304 | tf_op jit(solution)/shard_map/all_to_all | solution.py:42
  138.1 17.9 %all-to-all-start.3 = ((bf16[8,4,128,128]{3,2,0,1:T(8,128)(2,1)}), bf16[8,4,128,128]{3,2,0,1:T(8,128)(2,1)S(1)}, u32[]{:S(2)}, u32[]{:S(2)}) async-start(bf16[8,4,128,128]{3,2,0,1:T(8,128)(2,1)} %copy.42), calls=%async_computation.3 | async-start | bytes 2097152 | tf_op jit(solution)/shard_map/all_to_all | solution.py:35
  163.9 1.2 copy-start.4
  172.9 1.2 copy-start.4
  181.8 1.2 copy-start.4
  190.7 1.2 copy-start.4
  199.6 1.2 copy-start.4
  208.5 1.2 copy-start.4
  217.4 1.2 copy-start.4
  226.3 1.2 copy-start.4
  259.6 50.9 %all-to-all-start.5 = ((bf16[8,4,128,128]{3,2,0,1:T(8,128)(2,1)}), bf16[8,4,128,128]{3,2,0,1:T(8,128)(2,1)S(1)}, u32[]{:S(2)}, u32[]{:S(2)}) async-start(bf16[8,4,128,128]{3,2,0,1:T(8,128)(2,1)} %copy.47), calls=%async_computation.5 | async-start | bytes 2097152 | tf_op jit(solution)/shard_map/all_to_all | solution.py:79
where the time goes:
time: 328 us; the launch traced here: 327 us
  local copies, waits for them, and re-layouts  107 us (33%)
  blocking collectives  70.1 us (21%)
  other arithmetic  60 us (18%)
  waiting for transfers between devices  42.1 us (13%)
  starting transfers between devices  23.6 us (7%)
  matrix products  15.4 us (5%)
  loops' own time  5.75 us (2%)
    psum x1, blocking collectives, on_device(): overall = lax.psum(duplicate_total, ('wide', 'narrow'))  40.9 us
    reduce_or x8, other arithmetic, full_block(): jnp.any(earlier, axis=1).astype(jnp.float32)  33 us
    all_to_all x1, blocking collectives, on_device(): lax.all_to_all(back_rows, 'wide', split_axis=0, concat_axis=0, tiled=True)  29.2 us
    all_to_all x1, waiting for transfers between devices, on_device(): lax.all_to_all(sent_rows, 'wide', split_axis=0, concat_axis=0, tiled=True)  24.8 us
    gather x1, local copies, waits for them, and re-layouts, on_device(): live[sort_order].reshape(shaped)  23 us
    gather x1, local copies, waits for them, and re-layouts, on_device(): second_key[sort_order].reshape(shaped)  23 us
    gather x1, local copies, waits for them, and re-layouts, on_device(): first_key[sort_order].reshape(shaped)  23 us
    dot_general x8, matrix products, full_block(): jnp.dot(same.astype(jnp.bfloat16), flat_rows, preferred_element_type=jnp....  15.4 us
  transfers between devices with their start and end apart: 5, of which 3 were waited for; matrix products, arithmetic and copies ran while one was open for 7% of the time, Pallas kernels for 0%

commit v1 on v0

--- a/solution.py
+++ b/solution.py
@@ -2,6 +2,30 @@
 import jax.numpy as jnp
 from jax import lax
 from jax.sharding import PartitionSpec as P
+
+
+def cut_along(x, dim, size):
+    shape = x.shape
+    blocks = x.reshape(*shape[:dim], size, shape[dim] // size, *shape[dim + 1 :])
+    return jnp.moveaxis(blocks, dim, 0)
+
+
+def joined_along(blocks, dim):
+    blocks = jnp.moveaxis(blocks, 0, dim)
+    shape = blocks.shape
+    return blocks.reshape(*shape[:dim], shape[dim] * shape[dim + 1], *shape[dim + 2 :])
+
+
+def rotated_exchange(array, axis, split_dim, concat_dim):
+    count, here = (lax.axis_size(axis), lax.axis_index(axis))
+    parts = cut_along(array, split_dim, count)
+    out = parts
+    for step in range(1, count):
+        target, source = ((here + step) % count, (here - step) % count)
+        sent = lax.dynamic_index_in_dim(parts, target, 0)
+        other = lax.ppermute(sent, axis, [(i, (i + step) % count) for i in range(count)])
+        out = lax.dynamic_update_slice_in_dim(out, other, source, axis=0)
+    return joined_along(out, concat_dim)
 
 
 def pair_mask(row_one, row_two, row_live, col_one, col_two, col_live):
@@ -77,11 +101,7 @@
     )
     back_rows = group_means.reshape(wide_count, narrow_count, slot_rows, feature_cols)
     returned = lax.all_to_all(
-        lax.all_to_all(back_rows, "wide", split_axis=0, concat_axis=0, tiled=True),
-        "narrow",
-        split_axis=1,
-        concat_axis=1,
-        tiled=True,
+        rotated_exchange(back_rows, "wide", 0, 0), "narrow", split_axis=1, concat_axis=1, tiled=True
     )
     group_mean = returned.reshape(row_count, feature_cols)[inverse]
     overall = lax.psum(duplicate_total, ("wide", "narrow"))

time: 328 us -> 316 us (0.963)
  blocking collectives: 70.1 us -> 48.5 us
  waiting for transfers between devices: 42.1 us -> 51.9 us
  starting transfers between devices: 23.6 us -> 32.7 us
  matrix products: 15.4 us -> 10.6 us
    all_to_all x1 -> x0, blocking collectives: 29.2 us -> none  [on_device(): lax.all_to_all(back_rows, 'wide', split_axis=0, concat_axis=0, tiled=True)]
    ppermute x0 -> x7, waiting for transfers between devices: none -> 9.96 us  [rotated_exchange(): lax.ppermute(sent, axis, [(i, (i + step) % count) for i in range(count)])]
    ppermute x0 -> x7, starting transfers between devices: none -> 9.12 us  [rotated_exchange(): lax.ppermute(sent, axis, [(i, (i + step) % count) for i in range(count)])]
    psum x1, blocking collectives: 40.9 us -> 48.5 us  [on_device(): overall = lax.psum(duplicate_total, ('wide', 'narrow'))]
    dot_general x8, matrix products: 15.4 us -> 10.6 us  [full_block(): jnp.dot(same.astype(jnp.bfloat16), flat_rows, preferred_element_type=jnp....]
  transfers between devices with their start and end apart: 5 -> 12, of which waited for: 3 -> 6; matrix products, arithmetic and copies ran while one was open for 7% -> 7% of each run, Pallas kernels for 0% -> 0%
where the time goes in v1:
time: 316 us; the launch traced here: 315 us
  local copies, waits for them, and re-layouts  104 us (33%)
  other arithmetic  59.5 us (19%)
  waiting for transfers between devices  51.9 us (16%)
  blocking collectives  48.5 us (15%)
  starting transfers between devices  32.7 us (10%)
  matrix products  10.6 us (3%)
  loops' own time  5.6 us (2%)
    psum x1, blocking collectives, on_device(): overall = lax.psum(duplicate_total, ('wide', 'narrow'))  48.5 us
    reduce_or x8, other arithmetic, full_block(): jnp.any(earlier, axis=1).astype(jnp.float32)  32.9 us
    all_to_all x1, waiting for transfers between devices, on_device(): lax.all_to_all(sent_rows, 'wide', split_axis=0, concat_axis=0, tiled=True)  24.8 us
    gather x1, local copies, waits for them, and re-layouts, on_device(): live[sort_order].reshape(shaped)  23 us
    gather x1, local copies, waits for them, and re-layouts, on_device(): second_key[sort_order].reshape(shaped)  23 us
    gather x1, local copies, waits for them, and re-layouts, on_device(): first_key[sort_order].reshape(shaped)  23 us
    gather x1, local copies, waits for them, and re-layouts, on_device(): payload[sort_order]  15 us
    gather x1, local copies, waits for them, and re-layouts, on_device(): group_mean = returned.reshape(row_count, feature_cols)[inverse]  15 us
  transfers between devices with their start and end apart: 12, of which 6 were waited for; matrix products, arithmetic and copies ran while one was open for 7% of the time, Pallas kernels for 0%

profile of v1, /device:TPU:0, one launch (start us, length us, event | category | flops | bytes accessed | tf_op | source)
XLA Modules:
  0.0 315.4 jit_solution(13931927079038408655)
XLA Ops:
  0.7 0.8 multiply_add_fusion
  1.5 5.8 %sort.31 = (s32[4096]{0:T(1024)}, s32[4096]{0:T(1024)S(1)}) sort(s32[4096]{0:T(1024)S(1)} %multiply_add_fusion, s32[4096]{0:T(1024)S(1)} %iota.19), dimensions={0}, to_apply=%region_0.0 | sort | flops 49152 | bytes 65536 | tf_op jit(solution)/shard_map/jit(argsort)/sort | solution.py:46
  7.3 23.0 %gather_fusion.2 = s32[4096]{0:T(1024)S(1)} fusion(s32[4096]{0:T(1024)S(1)} %copy-done.1, s32[4096]{0:T(1024)S(1)} %fusion.6), kind=kCustom, calls=%fused_computation.2 | custom fusion | bytes 49152 | tf_op jit(solution)/shard_map/gather | solution.py:54
  30.4 23.0 %gather_fusion.1 = s32[4096]{0:T(1024)S(1)} fusion(s32[4096]{0:T(1024)S(1)} %copy-done.2, s32[4096]{0:T(1024)S(1)} %fusion.6), kind=kCustom, calls=%fused_computation.1 | custom fusion | bytes 49152 | tf_op jit(solution)/shard_map/gather | solution.py:53
  53.4 23.0 %gather_fusion = s32[4096]{0:T(1024)S(1)} fusion(s32[4096]{0:T(1024)S(1)} %copy-done.3, s32[4096]{0:T(1024)S(1)} %fusion.6), kind=kCustom, calls=%fused_computation | custom fusion | bytes 49152 | tf_op jit(solution)/shard_map/gather | solution.py:52
  76.4 0.6 pad_add_fusion
  77.1 7.3 %all-to-all-start = ((s32[8,4,3,128]{3,1,2,0:T(4,128)}), s32[8,4,3,128]{3,1,2,0:T(4,128)S(1)}, u32[]{:S(2)}, u32[]{:S(2)}) async-start(s32[8,4,3,128]{3,1,2,0:T(4,128)} %pad_add_fusion), calls=%async_computation | async-start | bytes 98304 | tf_op jit(solution)/shard_map/all_to_all | solution.py:67
  84.4 15.0 %gather_fusion.3 = bf16[4096,128]{1,0:T(8,128)(2,1)} fusion(bf16[4096,128]{1,0:T(8,128)(2,1)S(1)} %copy-done, s32[4096]{0:T(1024)S(1)} %fusion.6), kind=kCustom, calls=%fused_computation.3 | custom fusion | bytes 2113536 | tf_op jit(solution)/shard_map/gather | solution.py:48
  99.4 6.0 %all-to-all-start.2 = ((bf16[8,4,128,128]{3,2,1,0:T(8,128)(2,1)}), bf16[8,4,128,128]{3,2,1,0:T(8,128)(2,1)S(1)}, u32[]{:S(2)}, u32[]{:S(2)}) async-start(bf16[8,4,128,128]{3,2,1,0:T(8,128)(2,1)} %bitcast.6), calls=%async_computation.2 | async-start | bytes 2097152 | tf_op jit(solution)/shard_map/all_to_all | solution.py:60
  105.4 0.6 copy.58
  106.0 24.8 %all-to-all-done.2 = bf16[8,4,128,128]{3,2,1,0:T(8,128)(2,1)S(1)} async-done(((bf16[8,4,128,128]{3,2,1,0:T(8,128)(2,1)}), bf16[8,4,128,128]{3,2,1,0:T(8,128)(2,1)S(1)}, u32[]{:S(2)}, u32[]{:S(2)}) %all-to-all-start.2) | async-done | bytes 1048608 | tf_op jit(solution)/shard_map/all_to_all | solution.py:60
  130.8 3.3 %all-to-all-start.1 = ((s32[8,4,3,128]{3,0,2,1:T(8,128)}), s32[8,4,3,128]{3,0,2,1:T(8,128)S(1)}, u32[]{:S(2)}, u32[]{:S(2)}) async-start(s32[8,4,3,128]{3,0,2,1:T(8,128)} %copy.58), calls=%async_computation.1 | async-start | bytes 98304 | tf_op jit(solution)/shard_map/all_to_all | solution.py:66
  134.1 1.0 copy.62
  135.1 3.0 all-to-all-done.1
  138.1 3.5 %all-to-all-start.3 = ((bf16[8,4,128,128]{3,2,0,1:T(8,128)(2,1)}), bf16[8,4,128,128]{3,2,0,1:T(8,128)(2,1)S(1)}, u32[]{:S(2)}, u32[]{:S(2)}) async-start(bf16[8,4,128,128]{3,2,0,1:T(8,128)(2,1)} %copy.62), calls=%async_computation.3 | async-start | bytes 2097152 | tf_op jit(solution)/shard_map/all_to_all | solution.py:59
  141.8 14.2 %all-to-all-done.3 = bf16[8,4,128,128]{3,2,0,1:T(8,128)(2,1)S(1)} async-done(((bf16[8,4,128,128]{3,2,0,1:T(8,128)(2,1)}), bf16[8,4,128,128]{3,2,0,1:T(8,128)(2,1)S(1)}, u32[]{:S(2)}, u32[]{:S(2)}) %all-to-all-start.3) | async-done | bytes 1048608 | tf_op jit(solution)/shard_map/all_to_all | solution.py:59
  156.1 0.1 broadcast_in_dim.30
  156.3 63.9 %while.16 = (s32[]{:T(128)}, bf16[4096,128]{1,0:T(8,128)(2,1)S(1)}, f32[]{:T(128)}, s32[4096]{0:T(1024)S(1)}, s32[8,4,1,128]{3,2,1,0:T(1,128)S(1)}, /*index=5*/s...) while((s32[]{:T(128)}, bf16[4096,128]{1,0:T(8,128)(2,1)S(1)}, ...), condition=%wide.region_5.6_spmd.clone, body=%wide.region_1.5_spmd.clone.sunk | while | flops 557979136 | bytes 7557343 | solution.py:99
  156.6 4.1 %fusion.17 = (pred[512]{0:T(512)(128)(4,1)S(1)}, pred[512,4096]{1,0:T(32,128)(4,1)S(1)}) fusion(s32[512]{0:T(512)S(1)} %iota_add_fusion.2, pred[4096]{0:T(1024)(128)(4,1)S(1)} %bitcast.49, pred[512]{0:T(512)(128)(4,1)S(1)} %dynamic-slice_compare_fusion.2, s32[4096]{0:T(1024)S(1)} %bitcast.48, s32[512]{0:T(512)S(1)} %dynamic_slice.65, ...), kind=kLoop, calls=%fused_computation.9.clone.1 | loop fusion | flops 16776704 | bytes 2141184 | tf_op jit(solution)/shard_map/while/body/eval_jaxpr/reduce_or | solution.py:93
  160.7 1.0 convert_reduce_fusion.4
  161.7 1.3 fusion.18
  163.0 0.6 convert_reduce_fusion.5
  164.5 4.1 %fusion.17 = (pred[512]{0:T(512)(128)(4,1)S(1)}, pred[512,4096]{1,0:T(32,128)(4,1)S(1)}) fusion(s32[512]{0:T(512)S(1)} %iota_add_fusion.2, pred[4096]{0:T(1024)(128)(4,1)S(1)} %bitcast.49, pred[512]{0:T(512)(128)(4,1)S(1)} %dynamic-slice_compare_fusion.2, s32[4096]{0:T(1024)S(1)} %bitcast.48, s32[512]{0:T(512)S(1)} %dynamic_slice.65, ...), kind=kLoop, calls=%fused_computation.9.clone.1 | loop fusion | flops 16776704 | bytes 2141184 | tf_op jit(solution)/shard_map/while/body/eval_jaxpr/reduce_or | solution.py:93
  168.7 1.0 convert_reduce_fusion.4
  169.7 1.3 fusion.18
  171.0 0.6 convert_reduce_fusion.5
  172.5 4.1 %fusion.17 = (pred[512]{0:T(512)(128)(4,1)S(1)}, pred[512,4096]{1,0:T(32,128)(4,1)S(1)}) fusion(s32[512]{0:T(512)S(1)} %iota_add_fusion.2, pred[4096]{0:T(1024)(128)(4,1)S(1)} %bitcast.49, pred[512]{0:T(512)(128)(4,1)S(1)} %dynamic-slice_compare_fusion.2, s32[4096]{0:T(1024)S(1)} %bitcast.48, s32[512]{0:T(512)S(1)} %dynamic_slice.65, ...), kind=kLoop, calls=%fused_computation.9.clone.1 | loop fusion | flops 16776704 | bytes 2141184 | tf_op jit(solution)/shard_map/while/body/eval_jaxpr/reduce_or | solution.py:93
  176.6 1.0 convert_reduce_fusion.4
  177.6 1.3 fusion.18
  179.0 0.6 convert_reduce_fusion.5
  180.5 4.1 %fusion.17 = (pred[512]{0:T(512)(128)(4,1)S(1)}, pred[512,4096]{1,0:T(32,128)(4,1)S(1)}) fusion(s32[512]{0:T(512)S(1)} %iota_add_fusion.2, pred[4096]{0:T(1024)(128)(4,1)S(1)} %bitcast.49, pred[512]{0:T(512)(128)(4,1)S(1)} %dynamic-slice_compare_fusion.2, s32[4096]{0:T(1024)S(1)} %bitcast.48, s32[512]{0:T(512)S(1)} %dynamic_slice.65, ...), kind=kLoop, calls=%fused_computation.9.clone.1 | loop fusion | flops 16776704 | bytes 2141184 | tf_op jit(solution)/shard_map/while/body/eval_jaxpr/reduce_or | solution.py:93
  184.6 1.0 convert_reduce_fusion.4
  185.6 1.3 fusion.18
  187.0 0.6 convert_reduce_fusion.5
  188.5 4.1 %fusion.17 = (pred[512]{0:T(512)(128)(4,1)S(1)}, pred[512,4096]{1,0:T(32,128)(4,1)S(1)}) fusion(s32[512]{0:T(512)S(1)} %iota_add_fusion.2, pred[4096]{0:T(1024)(128)(4,1)S(1)} %bitcast.49, pred[512]{0:T(512)(128)(4,1)S(1)} %dynamic-slice_compare_fusion.2, s32[4096]{0:T(1024)S(1)} %bitcast.48, s32[512]{0:T(512)S(1)} %dynamic_slice.65, ...), kind=kLoop, calls=%fused_computation.9.clone.1 | loop fusion | flops 16776704 | bytes 2141184 | tf_op jit(solution)/shard_map/while/body/eval_jaxpr/reduce_or | solution.py:93
  192.6 1.0 convert_reduce_fusion.4
  193.6 1.3 fusion.18
  194.9 0.6 convert_reduce_fusion.5
  196.5 4.1 %fusion.17 = (pred[512]{0:T(512)(128)(4,1)S(1)}, pred[512,4096]{1,0:T(32,128)(4,1)S(1)}) fusion(s32[512]{0:T(512)S(1)} %iota_add_fusion.2, pred[4096]{0:T(1024)(128)(4,1)S(1)} %bitcast.49, pred[512]{0:T(512)(128)(4,1)S(1)} %dynamic-slice_compare_fusion.2, s32[4096]{0:T(1024)S(1)} %bitcast.48, s32[512]{0:T(512)S(1)} %dynamic_slice.65, ...), kind=kLoop, calls=%fused_computation.9.clone.1 | loop fusion | flops 16776704 | bytes 2141184 | tf_op jit(solution)/shard_map/while/body/eval_jaxpr/reduce_or | solution.py:93
  200.6 1.0 convert_reduce_fusion.4
  201.6 1.3 fusion.18
  202.9 0.6 convert_reduce_fusion.5
  204.5 4.1 %fusion.17 = (pred[512]{0:T(512)(128)(4,1)S(1)}, pred[512,4096]{1,0:T(32,128)(4,1)S(1)}) fusion(s32[512]{0:T(512)S(1)} %iota_add_fusion.2, pred[4096]{0:T(1024)(128)(4,1)S(1)} %bitcast.49, pred[512]{0:T(512)(128)(4,1)S(1)} %dynamic-slice_compare_fusion.2, s32[4096]{0:T(1024)S(1)} %bitcast.48, s32[512]{0:T(512)S(1)} %dynamic_slice.65, ...), kind=kLoop, calls=%fused_computation.9.clone.1 | loop fusion | flops 16776704 | bytes 2141184 | tf_op jit(solution)/shard_map/while/body/eval_jaxpr/reduce_or | solution.py:93
  208.6 1.0 convert_reduce_fusion.4
  209.6 1.3 fusion.18
  210.9 0.6 convert_reduce_fusion.5
  212.4 4.1 %fusion.17 = (pred[512]{0:T(512)(128)(4,1)S(1)}, pred[512,4096]{1,0:T(32,128)(4,1)S(1)}) fusion(s32[512]{0:T(512)S(1)} %iota_add_fusion.2, pred[4096]{0:T(1024)(128)(4,1)S(1)} %bitcast.49, pred[512]{0:T(512)(128)(4,1)S(1)} %dynamic-slice_compare_fusion.2, s32[4096]{0:T(1024)S(1)} %bitcast.48, s32[512]{0:T(512)S(1)} %dynamic_slice.65, ...), kind=kLoop, calls=%fused_computation.9.clone.1 | loop fusion | flops 16776704 | bytes 2141184 | tf_op jit(solution)/shard_map/while/body/eval_jaxpr/reduce_or | solution.py:93
  216.6 1.0 convert_reduce_fusion.4
  217.6 1.3 fusion.18
  218.9 0.6 convert_reduce_fusion.5
  220.2 0.1 constant_dynamic-slice_fusion
  220.3 1.3 collective-permute-start
  221.5 1.7 collective-permute-start.2
  223.3 2.3 collective-permute-start.3
  225.6 1.8 collective-permute-start.4
  227.4 2.2 collective-permute-done
  229.6 0.2 collective-permute-done.1
  229.8 2.0 collective-permute-start.6
  231.8 7.5 %collective-permute-done.2 = bf16[1,1,4,128,128]{4,3,2,1,0:T(8,128)(2,1)S(1)} collective-permute-done((bf16[1,1,4,128,128]{4,3,2,1,0:T(8,128)(2,1)S(1)}, bf16[1,1,4,128,128]{4,3,2,1,0:T(8,128)(2,1)S(1)}, u32[]{:S(2)}, u32[]{:S(2)}) %collective-permute-start.2) | collective-permute-done | bytes 131104 | tf_op jit(solution)/shard_map/ppermute | solution.py:26
  239.6 1.0 copy.67
  240.6 3.5 %all-to-all-start.4 = ((bf16[8,4,128,128]{3,2,0,1:T(8,128)(2,1)}), bf16[8,4,128,128]{3,2,0,1:T(8,128)(2,1)S(1)}, u32[]{:S(2)}, u32[]{:S(2)}) async-start(bf16[8,4,128,128]{3,2,0,1:T(8,128)(2,1)} %copy.67), calls=%async_computation.4 | async-start | bytes 2097152 | tf_op jit(solution)/shard_map/all_to_all | solution.py:103
  244.1 5.8 %sort.32 = (s32[4096]{0:T(1024)}, s32[4096]{0:T(1024)S(1)}) sort(s32[4096]{0:T(1024)S(1)} %get-tuple-element.189, s32[4096]{0:T(1024)S(1)} %iota.21), dimensions={0}, to_apply=%region_6.7 | sort | flops 49152 | bytes 65536 | tf_op jit(solution)/shard_map/jit(argsort)/sort | solution.py:47
  249.9 48.5 %psum.7 = f32[]{:T(128)} all-reduce(f32[]{:T(128)} %get-tuple-element.192), channel_id=1, replica_groups=mesh['wide'=8,'narrow'=4] {'wide','narrow'}, use_global_device_ids=true, to_apply=%region_7.8 | all-reduce | flops 1 | bytes 8 | tf_op jit(solution)/shard_map/psum | solution.py:107
  299.2 15.0 %gather_fusion.4 = bf16[4096,128]{1,0:T(8,128)(2,1)} fusion(bf16[4096,128]{1,0:T(8,128)(2,1)S(1)} %bitcast.40, s32[4096]{0:T(1024)S(1)} %fusion.7), kind=kCustom, calls=%fused_computation.4 | custom fusion | bytes 2113536 | tf_op jit(solution)/shard_map/gather | solution.py:106
  (83 shorter events, 2.5 us)
Async XLA Ops:
  0.6 83.7 %copy-start = (bf16[4096,128]{1,0:T(8,128)(2,1)S(1)}, bf16[4096,128]{1,0:T(8,128)(2,1)}, u32[]{:S(2)}) copy-start(bf16[4096,128]{1,0:T(8,128)(2,1)} %param.8) | copy-start | bytes 3145732
  0.6 6.6 %copy-start.1 = (s32[4096]{0:T(1024)S(1)}, s32[4096]{0:T(1024)}, u32[]{:S(2)}) copy-start(s32[4096]{0:T(1024)} %param.11) | copy-start | bytes 49156
  7.3 23.1 %copy-start.2 = (s32[4096]{0:T(1024)S(1)}, s32[4096]{0:T(1024)}, u32[]{:S(2)}) copy-start(s32[4096]{0:T(1024)} %param.10) | copy-start | bytes 49156
  30.3 23.1 %copy-start.3 = (s32[4096]{0:T(1024)S(1)}, s32[4096]{0:T(1024)}, u32[]{:S(2)}) copy-start(s32[4096]{0:T(1024)} %param.9) | copy-start | bytes 49156
  77.1 22.3 %all-to-all-start = ((s32[8,4,3,128]{3,1,2,0:T(4,128)}), s32[8,4,3,128]{3,1,2,0:T(4,128)S(1)}, u32[]{:S(2)}, u32[]{:S(2)}) async-start(s32[8,4,3,128]{3,1,2,0:T(4,128)} %pad_add_fusion), calls=%async_computation | async-start | bytes 98304 | tf_op jit(solution)/shard_map/all_to_all | solution.py:67
  99.4 31.4 %all-to-all-start.2 = ((bf16[8,4,128,128]{3,2,1,0:T(8,128)(2,1)}), bf16[8,4,128,128]{3,2,1,0:T(8,128)(2,1)S(1)}, u32[]{:S(2)}, u32[]{:S(2)}) async-start(bf16[8,4,128,128]{3,2,1,0:T(8,128)(2,1)} %bitcast.6), calls=%async_computation.2 | async-start | bytes 2097152 | tf_op jit(solution)/shard_map/all_to_all | solution.py:60
  130.8 7.3 %all-to-all-start.1 = ((s32[8,4,3,128]{3,0,2,1:T(8,128)}), s32[8,4,3,128]{3,0,2,1:T(8,128)S(1)}, u32[]{:S(2)}, u32[]{:S(2)}) async-start(s32[8,4,3,128]{3,0,2,1:T(8,128)} %copy.58), calls=%async_computation.1 | async-start | bytes 98304 | tf_op jit(solution)/shard_map/all_to_all | solution.py:66
  138.1 17.9 %all-to-all-start.3 = ((bf16[8,4,128,128]{3,2,0,1:T(8,128)(2,1)}), bf16[8,4,128,128]{3,2,0,1:T(8,128)(2,1)S(1)}, u32[]{:S(2)}, u32[]{:S(2)}) async-start(bf16[8,4,128,128]{3,2,0,1:T(8,128)(2,1)} %copy.62), calls=%async_computation.3 | async-start | bytes 2097152 | tf_op jit(solution)/shard_map/all_to_all | solution.py:59
  220.3 9.3 %collective-permute-start = (bf16[1,1,4,128,128]{4,3,2,1,0:T(8,128)(2,1)S(1)}, bf16[1,1,4,128,128]{4,3,2,1,0:T(8,128)(2,1)S(1)}, u32[]{:S(2)}, u32[]{:S(2)}) collective-permute-start(bf16[1,1,4,128,128]{4,3,2,1,0:T(8,128)(2,1)S(1)} %get-tuple-element.293), channel_id=1, source_target_pairs={{0,4},{4,8},{8,12},{12,16},{16,20},{20,24},{24,28},{28,0},{1,5},{5... | collective-permute-start | bytes 393224 | tf_op jit(solution)/shard_map/ppermute | solution.py:26
  221.5 8.3 %collective-permute-start.1 = (bf16[1,1,4,128,128]{4,3,2,1,0:T(8,128)(2,1)S(1)}, bf16[1,1,4,128,128]{4,3,2,1,0:T(8,128)(2,1)S(1)}, u32[]{:S(2)}, u32[]{:S(2)}) collective-permute-start(bf16[1,1,4,128,128]{4,3,2,1,0:T(8,128)(2,1)S(1)} %get-tuple-element.292), channel_id=1, source_target_pairs={{0,8},{4,12},{8,16},{12,20},{16,24},{20,28},{24,0},{28,4},{1,9},{5... | collective-permute-start | bytes 393224 | tf_op jit(solution)/shard_map/ppermute | solution.py:26
  221.5 17.8 %collective-permute-start.2 = (bf16[1,1,4,128,128]{4,3,2,1,0:T(8,128)(2,1)S(1)}, bf16[1,1,4,128,128]{4,3,2,1,0:T(8,128)(2,1)S(1)}, u32[]{:S(2)}, u32[]{:S(2)}) collective-permute-start(bf16[1,1,4,128,128]{4,3,2,1,0:T(8,128)(2,1)S(1)} %get-tuple-element.291), channel_id=1, source_target_pairs={{0,12},{4,16},{8,20},{12,24},{16,28},{20,0},{24,4},{28,8},{1,13},{... | collective-permute-start | bytes 393224 | tf_op jit(solution)/shard_map/ppermute | solution.py:26
  223.3 16.1 %collective-permute-start.3 = (bf16[1,1,4,128,128]{4,3,2,1,0:T(8,128)(2,1)S(1)}, bf16[1,1,4,128,128]{4,3,2,1,0:T(8,128)(2,1)S(1)}, u32[]{:S(2)}, u32[]{:S(2)}) collective-permute-start(bf16[1,1,4,128,128]{4,3,2,1,0:T(8,128)(2,1)S(1)} %get-tuple-element.290), channel_id=1, source_target_pairs={{0,16},{4,20},{8,24},{12,28},{16,0},{20,4},{24,8},{28,12},{1,17},{... | collective-permute-start | bytes 393224 | tf_op jit(solution)/shard_map/ppermute | solution.py:26
  225.6 13.8 %collective-permute-start.4 = (bf16[1,1,4,128,128]{4,3,2,1,0:T(8,128)(2,1)S(1)}, bf16[1,1,4,128,128]{4,3,2,1,0:T(8,128)(2,1)S(1)}, u32[]{:S(2)}, u32[]{:S(2)}) collective-permute-start(bf16[1,1,4,128,128]{4,3,2,1,0:T(8,128)(2,1)S(1)} %get-tuple-element.289), channel_id=1, source_target_pairs={{0,20},{4,24},{8,28},{12,0},{16,4},{20,8},{24,12},{28,16},{1,21},{... | collective-permute-start | bytes 393224 | tf_op jit(solution)/shard_map/ppermute | solution.py:26
  229.6 9.9 %collective-permute-start.5 = (bf16[1,1,4,128,128]{4,3,2,1,0:T(8,128)(2,1)S(1)}, bf16[1,1,4,128,128]{4,3,2,1,0:T(8,128)(2,1)S(1)}, u32[]{:S(2)}, u32[]{:S(2)}) collective-permute-start(bf16[1,1,4,128,128]{4,3,2,1,0:T(8,128)(2,1)S(1)} %get-tuple-element.288), channel_id=1, source_target_pairs={{0,24},{4,28},{8,0},{12,4},{16,8},{20,12},{24,16},{28,20},{1,25},{... | collective-permute-start | bytes 393224 | tf_op jit(solution)/shard_map/ppermute | solution.py:26
  229.8 9.7 %collective-permute-start.6 = (bf16[1,1,4,128,128]{4,3,2,1,0:T(8,128)(2,1)S(1)}, bf16[1,1,4,128,128]{4,3,2,1,0:T(8,128)(2,1)S(1)}, u32[]{:S(2)}, u32[]{:S(2)}) collective-permute-start(bf16[1,1,4,128,128]{4,3,2,1,0:T(8,128)(2,1)S(1)} %get-tuple-element.287), channel_id=1, source_target_pairs={{0,28},{4,0},{8,4},{12,8},{16,12},{20,16},{24,20},{28,24},{1,29},{... | collective-permute-start | bytes 393224 | tf_op jit(solution)/shard_map/ppermute | solution.py:26
  240.6 58.5 %all-to-all-start.4 = ((bf16[8,4,128,128]{3,2,0,1:T(8,128)(2,1)}), bf16[8,4,128,128]{3,2,0,1:T(8,128)(2,1)S(1)}, u32[]{:S(2)}, u32[]{:S(2)}) async-start(bf16[8,4,128,128]{3,2,0,1:T(8,128)(2,1)} %copy.67), calls=%async_computation.4 | async-start | bytes 2097152 | tf_op jit(solution)/shard_map/all_to_all | solution.py:103
